TPU v7x, 256 devices: a whole 4x4x8 slice. The times are simulated.
256 devices in a mesh: expert: 8 (over x, y_lo), tensor: 16 (over y_hi, z), dp: 2 (over core).
Axes of the slice: x: 4, y: 4 (y_hi: 2, y_lo: 2; y = y_hi * 2 + y_lo), z: 8, core: 2. Of those that a mesh axis runs over, the one named last changes fastest.
Arguments:
- x_real: bfloat16 [4096, 2048], P(('expert', 'dp'), 'tensor'), may hold values from -6 to 6
- routes_real: int32 [4096, 2], P(('expert', 'dp')), may hold values from 0 to 7, all different within a row; in each aligned block of 256 rows (0 to 255, 256 to 511, ...) at most 128 rows name the same one
- gates_real: float32 [4096, 2], P(('expert', 'dp')), may hold values from 0.2 to 1
- up_real: bfloat16 [8, 2048, 8192], P('expert', None, 'tensor'), may hold values from -0.125 to 0.125
- down_real: bfloat16 [8, 8192, 2048], P('expert', 'tensor'), may hold values from -0.0625 to 0.0625
- x_fake: bfloat16 [4096, 2048], P(('expert', 'dp'), 'tensor'), may hold values from -6 to 6
- routes_fake: int32 [4096, 2], P(('expert', 'dp')), may hold values from 0 to 7, all different within a row; in each aligned block of 256 rows (0 to 255, 256 to 511, ...) at most 128 rows name the same one
- gates_fake: float32 [4096, 2], P(('expert', 'dp')), may hold values from 0.2 to 1
- cotangent: bfloat16 [4096, 2048], P(('expert', 'dp'), 'tensor'), may hold values from -6 to 6
- up_fake: bfloat16 [8, 2048, 8192], P('expert', None, 'tensor'), may hold values from -0.125 to 0.125
- down_fake: bfloat16 [8, 8192, 2048], P('expert', 'tensor'), may hold values from -0.0625 to 0.0625
Outputs:
- real_out: bfloat16 [4096, 2048], P(('expert', 'dp'), 'tensor')
- grad_up: bfloat16 [8, 2048, 8192], P('expert', 'dp', 'tensor')
- grad_down: bfloat16 [8, 8192, 2048], P('expert', 'tensor', 'dp')
Inputs may be any that keep to these rules, and one draw needn't show every extreme that they name: `routes_real`: each row names 2 different experts. In the 256 rows of one index of expert and dp no expert is named more than 128 times, and that bound is reached. `routes_fake`: each row names 2 different experts. In the 256 rows of one index of expert and dp no expert is named more than 128 times, and that bound is reached.
All inputs are finite; a program needn't handle non-finite values.
Results may differ from a plain program's by a relative error of at most 0.0058.
Values may be sent and summed in bfloat16 or wider, within the bound.
A program may use at most 128 MiB of HBM per device.

v0:
```python
import jax
import jax.numpy as jnp
from jax import lax
from jax.sharding import Mesh
from jax.sharding import PartitionSpec as P

TENSOR = ("tensor_0", "tensor_1")
slope_const = 0.7978845608028654
cubic_coef = 0.044715


def in_order(pieces, dim):
    pieces = jnp.moveaxis(pieces, 0, dim)
    dims = pieces.shape
    return pieces.reshape(*dims[:dim], dims[dim] * dims[dim + 1], *dims[dim + 2 :])


def sent_to_all(x, axis):
    copies = jnp.broadcast_to(x, (lax.axis_size(axis), *x.shape))
    return lax.all_to_all(copies, axis, split_axis=0, concat_axis=0, tiled=True)


def gather_directly(x, axis, dim):
    return in_order(sent_to_all(x, axis), dim)


def reduced_to_own(pieces, axes, turns):
    dims = [lax.axis_size(a) for a in axes]
    pieces = pieces.reshape(*dims, *pieces.shape[1:])
    pieces = pieces.transpose(*turns, *range(len(axes), pieces.ndim))
    pieces = pieces.reshape(-1, *pieces.shape[len(axes) :])
    for k in turns:
        pieces = lax.psum_scatter(pieces, axes[k], scatter_dimension=0, tiled=True)
    return pieces[0]


def in_blocks(x, dim, length):
    dims = x.shape
    pieces = x.reshape(*dims[:dim], length, dims[dim] // length, *dims[dim + 1 :])
    return jnp.moveaxis(pieces, dim, 0)


def sum_by_axis(x, axes, turns, dim):
    length = lax.axis_size(axes)
    return reduced_to_own(in_blocks(x, dim, length), axes, turns)


def sent_together(arrays, axis, dim, along):
    ends, at = ([], 0)
    for a in arrays[:-1]:
        at += a.shape[along]
        ends.append(at)
    both = jnp.concatenate(arrays, axis=along)
    return tuple(jnp.split(lax.all_gather(both, axis, axis=dim, tiled=True), ends, axis=along))


def in_one_piece(arrays, axis, split_dim, concat_dim, along):
    ends, at = ([], 0)
    for a in arrays[:-1]:
        at += a.shape[along]
        ends.append(at)
    both = jnp.concatenate(arrays, axis=along)
    return tuple(
        jnp.split(
            lax.all_to_all(both, axis, split_axis=split_dim, concat_axis=concat_dim, tiled=True),
            ends,
            axis=along,
        )
    )


def partner(value, axis, stride):
    mask = 2**stride
    pairs = [(source, source ^ mask) for source in range(lax.axis_size(axis))]
    return lax.ppermute(value, axis, pairs)


def gelu_tanh(value):
    return (
        0.5 * value * (1.0 + jnp.tanh(slope_const * (value + cubic_coef * value * value * value)))
    )


def gelu_slope(value):
    inner = jnp.tanh(slope_const * (value + cubic_coef * value * value * value))
    return 0.5 * (1.0 + inner) + 0.5 * value * (1.0 - inner * inner) * slope_const * (
        1.0 + 3.0 * cubic_coef * value * value
    )


def slot_index(routes, experts, capacity):
    labels = jnp.arange(experts, dtype=jnp.int32)
    hits = (routes[:, :, None] == labels[None, None, :]).astype(jnp.int32)
    per_token = jnp.sum(hits, axis=1)
    before = jnp.cumsum(per_token, axis=0) - per_token
    slots = jnp.sum(hits * before[:, None, :], axis=2)
    return routes * capacity + slots


def spread_matrix(position, total):
    columns = jnp.arange(total, dtype=jnp.int32)
    match = (position[:, :, None] == columns[None, None, :]).astype(jnp.float32)
    return jnp.sum(match, axis=1).astype(jnp.bfloat16)


def pick_matrix(position, total):
    columns = jnp.arange(total, dtype=jnp.int32)
    flat = position.reshape(-1)
    return (flat[:, None] == columns[None, :]).astype(jnp.bfloat16)


def to_slots(matrix, rows):
    return lax.dot_general(
        matrix, rows, (((0,), (0,)), ((), ())), preferred_element_type=jnp.float32
    )


def over_rows(left, right):
    return lax.dot_general(
        left, right, (((0,), (0,)), ((), ())), preferred_element_type=jnp.float32
    )


def scale_rows(gates, rows):
    scaled = gates[:, :, None] * rows[:, None, :].astype(jnp.float32)
    return scaled.astype(jnp.bfloat16).reshape(-1, rows.shape[1])


def on_device(
    x_real,
    routes_real,
    gates_real,
    up_real,
    down_real,
    x_fake,
    routes_fake,
    gates_fake,
    cotangent,
    up_fake,
    down_fake,
):
    experts = lax.axis_size("expert")
    tokens = x_real.shape[0]
    top = routes_real.shape[1]
    capacity = tokens // 2
    total = experts * capacity
    w_up = up_real[0]
    w_down = down_real[0]
    wf_up = up_fake[0]
    wf_down = down_fake[0]
    real_pos = slot_index(routes_real, experts, capacity)
    real_pick = spread_matrix(real_pos, total)
    whole = lax.all_gather(x_real, TENSOR, axis=1, tiled=True)
    fake_pos = slot_index(routes_fake, experts, capacity)
    fake_pick = spread_matrix(fake_pos, total)
    fake_flat = pick_matrix(fake_pos, total)
    part = x_fake.shape[1]
    sent_x = to_slots(fake_pick, x_fake).astype(jnp.bfloat16).reshape(experts, capacity, part)
    sent_d = (
        to_slots(fake_flat, scale_rows(gates_fake, cotangent))
        .astype(jnp.bfloat16)
        .reshape(experts, capacity, part)
    )
    got_x, got_d = in_one_piece((sent_x, sent_d), "expert", 0, 0, 1)
    both = jnp.concatenate((got_x.reshape(total, part), got_d.reshape(total, part)), axis=0)
    whole, both = lax.optimization_barrier((whole, both))
    both = lax.all_gather(both, TENSOR, axis=1, tiled=True)
    rows_x, rows_d = (both[:total], both[total:])
    width = whole.shape[1]
    sent = to_slots(real_pick, whole).astype(jnp.bfloat16).reshape(experts, capacity, width)
    arrived = lax.all_to_all(sent, "expert", split_axis=0, concat_axis=0, tiled=True)
    rows = arrived.reshape(total, width)
    pre_real = jnp.dot(rows, w_up, preferred_element_type=jnp.float32)
    hidden = gelu_tanh(pre_real).astype(jnp.bfloat16)
    partial_out = jnp.dot(hidden, w_down, preferred_element_type=jnp.float32).astype(jnp.bfloat16)
    returned = lax.all_to_all(
        partial_out.reshape(experts, capacity, width),
        "expert",
        split_axis=0,
        concat_axis=0,
        tiled=True,
    ).reshape(total, width)
    columns = jnp.arange(total, dtype=jnp.int32)
    match = (real_pos[:, :, None] == columns[None, None, :]).astype(jnp.float32)
    weights = jnp.sum(match * gates_real[:, :, None], axis=1)
    high = weights.astype(jnp.bfloat16)
    low = (weights - high.astype(jnp.float32)).astype(jnp.bfloat16)
    combined = jnp.dot(high, returned, preferred_element_type=jnp.float32) + jnp.dot(
        low, returned, preferred_element_type=jnp.float32
    )
    real_out = sum_by_axis(combined, TENSOR, (1, 0), 1).astype(jnp.bfloat16)
    pre_fake = jnp.dot(rows_x, wf_up, preferred_element_type=jnp.float32)
    act = gelu_tanh(pre_fake).astype(jnp.bfloat16)
    back_act = lax.dot_general(
        rows_d, wf_down, (((1,), (1,)), ((), ())), preferred_element_type=jnp.float32
    )
    dpre = (back_act * gelu_slope(pre_fake)).astype(jnp.bfloat16)
    mine = lax.axis_index("dp")
    half = rows_x.shape[1] // 2
    own_x = lax.dynamic_slice_in_dim(rows_x, mine * half, half, 1)
    other_x = lax.dynamic_slice_in_dim(rows_x, (1 - mine) * half, half, 1)
    own_d = lax.dynamic_slice_in_dim(rows_d, mine * half, half, 1)
    other_d = lax.dynamic_slice_in_dim(rows_d, (1 - mine) * half, half, 1)
    peer_x, peer_d, peer_act, peer_dpre = partner((other_x, other_d, act, dpre), "dp", 0)
    grad_in = over_rows(own_x, dpre) + over_rows(peer_x, peer_dpre)
    grad_out = over_rows(act, own_d) + over_rows(peer_act, peer_d)
    return (real_out, grad_in.astype(jnp.bfloat16)[None], grad_out.astype(jnp.bfloat16)[None])


def solution(mesh):
    split = Mesh(
        mesh.devices.reshape(mesh.shape["expert"], 2, 8, mesh.shape["dp"]),
        ("expert", "tensor_0", "tensor_1", "dp"),
    )
    placed = (
        P(("expert", "dp"), TENSOR),
        P(("expert", "dp"), None),
        P(("expert", "dp"), None),
        P("expert", None, TENSOR),
        P("expert", TENSOR, None),
        P(("expert", "dp"), TENSOR),
        P(("expert", "dp"), None),
        P(("expert", "dp"), None),
        P(("expert", "dp"), TENSOR),
        P("expert", None, TENSOR),
        P("expert", TENSOR, None),
    )
    return jax.shard_map(
        on_device,
        mesh=split,
        in_specs=placed,
        out_specs=(
            P(("expert", "dp"), TENSOR),
            P("expert", "dp", TENSOR),
            P("expert", TENSOR, "dp"),
        ),
        check_vma=False,
    )
```

profile of v0, /device:TPU:1, one launch (start us, length us, event | category | flops | bytes accessed | tf_op | source)
XLA Modules:
  0.0 432.8 jit_solution(8961847231231430238)
XLA Ops:
  7.2 0.0 copy-start
  7.2 0.0 all-gather.3.cloned.1.call-start
  7.2 0.7 all-gather.3.cloned.1.call-update
  7.9 0.7 convert_reduce_fusion.2
  8.6 0.6 reduce-window.16
  9.2 0.2 slice_reduce_fusion
  9.4 0.1 bitcast_subtract_fusion
  9.5 0.7 select_reduce_fusion.1
  10.2 0.7 multiply_add_fusion.2
  10.9 0.1 copy.30
  11.1 0.1 eq.86
  11.2 0.8 copy.31
  12.0 0.1 mul.132
  12.2 0.9 mul.134
  13.1 0.0 copy-start.7
  13.1 0.0 copy-start.8
  13.1 0.9 fusion.31
  14.0 0.3 convert_reduce_fusion
  14.3 0.3 convolution_convert_fusion.2
  14.6 0.8 pad_maximum_fusion
  15.5 5.8 %all-to-all-start = ((bf16[8,256,128]{2,1,0:T(8,128)(2,1)}), bf16[8,256,128]{2,1,0:T(8,128)(2,1)}, u32[]{:S(2)}, u32[]{:S(2)}) async-start(bf16[8,256,128]{2,1,0:T(8,128)(2,1)} %pad_maximum_fusion), calls=%async_computation | async-start | bytes 1048576 | tf_op jit(solution)/shard_map/all_to_all | solution.py:65
  21.3 0.0 reduce-scatter.3.cloned.1.call-start
  21.4 0.6 reduce-window.14
  22.0 0.2 slice_reduce_fusion.1
  22.2 0.1 bitcast_subtract_fusion.1
  22.3 1.2 select_reduce_fusion
  23.6 6.0 %all-to-all-done = bf16[8,256,128]{2,1,0:T(8,128)(2,1)} async-done(((bf16[8,256,128]{2,1,0:T(8,128)(2,1)}), bf16[8,256,128]{2,1,0:T(8,128)(2,1)}, u32[]{:S(2)}, u32[]{:S(2)}) %all-to-all-start) | async-done | bytes 524320 | tf_op jit(solution)/shard_map/all_to_all | solution.py:65
  29.6 1.1 fusion.50
  30.7 0.8 pad_maximum_fusion.1
  31.5 55.5 %all-gather.3.cloned.1.call-done = bf16[256,2048]{1,0:T(8,128)(2,1)} async-done(((bf16[256,128]{1,0:T(8,128)(2,1)}), bf16[256,2048]{1,0:T(8,128)(2,1)}) %all-gather.3.cloned.1.call-update) | async-done | bytes 1048592 | tf_op jit(solution)/shard_map/all_gather | solution.py:153
  87.0 2.7 convolution_convert_fusion.1
  89.7 48.2 %all_to_all.15 = bf16[8,128,2048]{2,1,0:T(8,128)(2,1)} all-to-all(bf16[8,128,2048]{2,1,0:T(8,128)(2,1)S(1)} %bitcast.72), channel_id=1, replica_groups=mesh['expert'=8,'tensor_0'=2,'tensor_1'=8,'dp'=2] {'expert'}, dimensions={0} | all-to-all | bytes 8388608 | tf_op jit(solution)/shard_map/all_to_all | solution.py:171
  137.9 9.6 %convolution_convert_fusion = bf16[1024,2048]{1,0:T(8,128)(2,1)} fusion(bf16[1,512,2048]{2,1,0:T(8,128)(2,1)S(1)} %copy-done, bf16[1024,2048]{1,0:T(8,128)(2,1)} %bitcast.77, bf16[1,2048,512]{2,1,0:T(8,128)(2,1)} %param.14), kind=kOutput, calls=%fused_computation | convolution fusion | flops 4301783040 | bytes 12582912 | tf_op jit(solution)/shard_map/dot_general | solution.py:175
  147.5 46.6 %all_to_all.16 = bf16[8,128,2048]{2,1,0:T(8,128)(2,1)S(1)} all-to-all(bf16[8,128,2048]{2,1,0:T(8,128)(2,1)} %bitcast.78), channel_id=1, replica_groups=mesh['expert'=8,'tensor_0'=2,'tensor_1'=8,'dp'=2] {'expert'}, dimensions={0} | all-to-all | bytes 8388608 | tf_op jit(solution)/shard_map/all_to_all | solution.py:176
  194.1 1.3 fusion.38
  195.4 1.3 fusion.24
  196.7 0.4 copy.33
  197.1 2.0 copy.32
  199.2 0.0 reduce-scatter.3.cloned.1.call-update
  199.2 0.0 all-gather.5.cloned.1.call-start
  199.2 0.7 all-gather.5.cloned.1.call-update
  199.9 0.0 reduce-scatter.5.cloned.1.call-start
  200.0 39.7 %reduce-scatter.3.cloned.1.call-done = f32[2,256,128]{2,1,0:T(8,128)} async-done(((f32[16,256,128]{2,1,0:T(8,128)}), f32[2,256,128]{2,1,0:T(8,128)}) %reduce-scatter.3.cloned.1.call-update) | async-done | bytes 262160 | tf_op jit(solution)/shard_map/reduce_scatter | solution.py:33
  239.7 0.0 reduce-scatter.5.cloned.1.call-update
  239.7 149.7 %all-gather.5.cloned.1.call-done = bf16[2048,2048]{1,0:T(8,128)(2,1)} async-done(((bf16[2048,128]{1,0:T(8,128)(2,1)}), bf16[2048,2048]{1,0:T(8,128)(2,1)}) %all-gather.5.cloned.1.call-update) | async-done | bytes 8388624 | tf_op jit(solution)/shard_map/all_gather | solution.py:167
  389.5 4.1 fusion.49
  393.6 0.2 constant_dynamic-slice_fusion.1
  393.9 4.4 %collective-permute-start = (bf16[1024,1024]{1,0:T(8,128)(2,1)S(1)}, bf16[1024,1024]{1,0:T(8,128)(2,1)}, u32[]{:S(2)}, u32[]{:S(2)}) collective-permute-start(bf16[1024,1024]{1,0:T(8,128)(2,1)S(1)} %constant_dynamic-slice_fusion.1), channel_id=1, source_target_pairs={{0,1},{1,0},{2,3},{3,2},{4,5},{5,4},{6,7},{7,6},{8,9},{9,8},{10,11... | collective-permute-start | bytes 6291464 | tf_op jit(solution)/shard_map/ppermute | solution.py:75
  398.3 1.6 constant_dynamic-slice_fusion
  399.9 1.6 collective-permute-start.3
  401.5 2.7 multiply_convert_fusion
  404.2 4.3 fusion.11
  408.5 3.4 collective-permute-start.1
  411.9 1.5 convert_bitcast_fusion
  413.4 0.0 collective-permute-start.2
  413.5 3.3 fusion.21
  416.7 1.3 fusion.19
  418.1 0.0 collective-permute-done.1
  418.1 0.0 collective-permute-done
  418.1 0.0 copy-start.1
  418.1 4.3 fusion.25
  422.4 0.0 collective-permute-done.2
  422.4 0.0 collective-permute-done.3
  422.4 3.9 fusion.26
  (26 shorter events, 0.2 us)
Async XLA Ops:
  7.2 130.7 %copy-start = (bf16[1,512,2048]{2,1,0:T(8,128)(2,1)S(1)}, bf16[1,512,2048]{2,1,0:T(8,128)(2,1)}, u32[]{:S(2)}) copy-start(bf16[1,512,2048]{2,1,0:T(8,128)(2,1)} %param.15) | copy-start | bytes 6291460
  7.2 7.1 %copy-start.6 = (bf16[256,128]{1,0:T(8,128)(2,1)S(1)}, bf16[256,128]{1,0:T(8,128)(2,1)}, u32[]{:S(2)}) copy-start(bf16[256,128]{1,0:T(8,128)(2,1)} %param.16) | copy-start | bytes 196612
  7.2 79.8 %all-gather.3.cloned.1.call-start = ((), (), s32[]{:S(2)}) async-start(), calls=%async_computation.5 | async-start | bytes 1114112 | tf_op jit(solution)/shard_map/all_gather | solution.py:153
  13.1 8.3 %copy-start.7 = (s32[256,2]{0,1:T(2,128)S(1)}, s32[256,2]{0,1:T(2,128)}, u32[]{:S(2)}) copy-start(s32[256,2]{0,1:T(2,128)} %param.12) | copy-start | bytes 6148
  13.1 9.2 %copy-start.8 = (f32[256,2]{0,1:T(2,128)S(1)}, f32[256,2]{0,1:T(2,128)}, u32[]{:S(2)}) copy-start(f32[256,2]{0,1:T(2,128)} %param.13) | copy-start | bytes 6148
  15.5 14.1 %all-to-all-start = ((bf16[8,256,128]{2,1,0:T(8,128)(2,1)}), bf16[8,256,128]{2,1,0:T(8,128)(2,1)}, u32[]{:S(2)}, u32[]{:S(2)}) async-start(bf16[8,256,128]{2,1,0:T(8,128)(2,1)} %pad_maximum_fusion), calls=%async_computation | async-start | bytes 1048576 | tf_op jit(solution)/shard_map/all_to_all | solution.py:65
  21.3 218.4 %reduce-scatter.3.cloned.1.call-start = ((), (), s32[]{:S(2)}) async-start(), calls=%async_computation.6 | async-start | bytes 2359296 | tf_op jit(solution)/shard_map/reduce_scatter | solution.py:33
  199.2 190.3 %all-gather.5.cloned.1.call-start = ((), (), s32[]{:S(2)}) async-start(), calls=%async_computation.8 | async-start | bytes 8912896 | tf_op jit(solution)/shard_map/all_gather | solution.py:167
  199.9 212.0 %reduce-scatter.5.cloned.1.call-start = ((), (), s32[]{:S(2)}) async-start(), calls=%async_computation.7 | async-start | bytes 393216 | tf_op jit(solution)/shard_map/reduce_scatter | solution.py:33
  389.5 12.0 %copy-start.9 = (bf16[1,2048,512]{2,1,0:T(8,128)(2,1)S(1)}, bf16[1,2048,512]{2,1,0:T(8,128)(2,1)}, u32[]{:S(2)}) copy-start(bf16[1,2048,512]{2,1,0:T(8,128)(2,1)} %param.20) | copy-start | bytes 6291460
  393.6 4.7 %copy-start.2 = (bf16[1024,2048]{1,0:T(8,128)(2,1)}, bf16[1024,2048]{1,0:T(8,128)(2,1)S(1)}, u32[]{:S(2)}) copy-start(bf16[1024,2048]{1,0:T(8,128)(2,1)S(1)} %get-tuple-element.9) | copy-start | bytes 12582916
  393.6 10.6 %copy-start.4 = (bf16[1024,2048]{1,0:T(8,128)(2,1)}, bf16[1024,2048]{1,0:T(8,128)(2,1)S(1)}, u32[]{:S(2)}) copy-start(bf16[1024,2048]{1,0:T(8,128)(2,1)S(1)} %get-tuple-element.10) | copy-start | bytes 12582916
  393.6 7.9 %copy-start.5 = (bf16[2048,2048]{1,0:T(8,128)(2,1)S(1)}, bf16[2048,2048]{1,0:T(8,128)(2,1)}, u32[]{:S(2)}) copy-start(bf16[2048,2048]{1,0:T(8,128)(2,1)} %all-gather.5.cloned.1.call-done) | copy-start | bytes 25165828
  393.9 24.2 %collective-permute-start = (bf16[1024,1024]{1,0:T(8,128)(2,1)S(1)}, bf16[1024,1024]{1,0:T(8,128)(2,1)}, u32[]{:S(2)}, u32[]{:S(2)}) collective-permute-start(bf16[1024,1024]{1,0:T(8,128)(2,1)S(1)} %constant_dynamic-slice_fusion.1), channel_id=1, source_target_pairs={{0,1},{1,0},{2,3},{3,2},{4,5},{5,4},{6,7},{7,6},{8,9},{9,8},{10,11... | collective-permute-start | bytes 6291464 | tf_op jit(solution)/shard_map/ppermute | solution.py:75
  399.9 4.4 %copy-start.10 = (bf16[1,512,2048]{2,1,0:T(8,128)(2,1)S(1)}, bf16[1,512,2048]{2,1,0:T(8,128)(2,1)}, u32[]{:S(2)}) copy-start(bf16[1,512,2048]{2,1,0:T(8,128)(2,1)} %param.21) | copy-start | bytes 6291460
  399.9 22.5 %collective-permute-start.3 = (bf16[1024,1024]{1,0:T(8,128)(2,1)}, bf16[1024,1024]{1,0:T(8,128)(2,1)}, u32[]{:S(2)}, u32[]{:S(2)}) collective-permute-start(bf16[1024,1024]{1,0:T(8,128)(2,1)} %constant_dynamic-slice_fusion), channel_id=1, source_target_pairs={{0,1},{1,0},{2,3},{3,2},{4,5},{5,4},{6,7},{7,6},{8,9},{9,8},{10,11... | collective-permute-start | bytes 6291464 | tf_op jit(solution)/shard_map/ppermute | solution.py:75
  408.5 9.5 %collective-permute-start.1 = (bf16[1024,512]{1,0:T(8,128)(2,1)}, bf16[1024,512]{1,0:T(8,128)(2,1)}, u32[]{:S(2)}, u32[]{:S(2)}) collective-permute-start(bf16[1024,512]{1,0:T(8,128)(2,1)} %fusion.11), channel_id=1, source_target_pairs={{0,1},{1,0},{2,3},{3,2},{4,5},{5,4},{6,7},{7,6},{8,9},{9,8},{10,11... | collective-permute-start | bytes 3145736 | tf_op jit(solution)/shard_map/ppermute | solution.py:75
  413.4 3.3 copy-start.3
  413.4 8.9 %collective-permute-start.2 = (bf16[1024,512]{1,0:T(8,128)(2,1)S(1)}, bf16[1024,512]{1,0:T(8,128)(2,1)S(1)}, u32[]{:S(2)}, u32[]{:S(2)}) collective-permute-start(bf16[1024,512]{1,0:T(8,128)(2,1)S(1)} %get-tuple-element.13), channel_id=1, source_target_pairs={{0,1},{1,0},{2,3},{3,2},{4,5},{5,4},{6,7},{7,6},{8,9},{9,8},{10,11... | collective-permute-start | bytes 3145736 | tf_op jit(solution)/shard_map/ppermute | solution.py:75
  418.1 8.1 %copy-start.1 = (bf16[1,512,2048]{2,1,0:T(8,128)(2,1)S(1)}, bf16[1,512,2048]{2,1,0:T(8,128)(2,1)}, u32[]{:S(2)}) copy-start(bf16[1,512,2048]{2,1,0:T(8,128)(2,1)} %param.15) | copy-start | bytes 6291460
Sparse Core Ops, SparseCore 0:
  10.5 76.4 all-gather.2
  199.3 40.3 reduce-scatter.2
  242.8 146.6 all-gather.4
  391.8 17.8 reduce-scatter.4
where the time goes:
time: 433 us
  waiting for transfers between devices  252 us (58%)
  blocking collectives  94.8 us (22%)
  matrix products  35.9 us (8%)
  starting transfers between devices  15.4 us (4%)
  between operations  14 us (3%)
  local copies, waits for them, and re-layouts  12.1 us (3%)
  other arithmetic  8.19 us (2%)
    all_gather x1, waiting for transfers between devices, on_device(): both = lax.all_gather(both, TENSOR, axis=1, tiled=True)  150 us
    all_gather x1, waiting for transfers between devices, on_device(): whole = lax.all_gather(x_real, TENSOR, axis=1, tiled=True)  55.5 us
    all_to_all x1, blocking collectives, on_device(): lax.all_to_all(sent, 'expert', split_axis=0, concat_axis=0, tiled=True)  48.2 us
    all_to_all x1, blocking collectives, on_device(): lax.all_to_all(partial_out.reshape(experts, capacity, width), 'expert', s...  46.6 us
    reduce_scatter x2, waiting for transfers between devices, reduced_to_own(): pieces = lax.psum_scatter(pieces, axes[k], scatter_dimension=0, tiled=True)  39.7 us
    dot_general x4, matrix products, over_rows(): lax.dot_general(left, right, (((0,), (0,)), ((), ())), preferred_element_...  12.7 us
    dot_general x1, matrix products, on_device(): jnp.dot(hidden, w_down, preferred_element_type=jnp.float32)  9.62 us
    ppermute x4, starting transfers between devices, partner(): return lax.ppermute(value, axis, pairs)  9.43 us
  transfers between devices with their start and end apart: 9, of which 4 were waited for; matrix products, arithmetic and copies ran while one was open for 8% of the time, Pallas kernels for 0%

commit v1 on v0

--- a/solution.py
+++ b/solution.py
@@ -1,3 +1,4 @@
+import functools
 import jax
 import jax.numpy as jnp
 from jax import lax
@@ -7,6 +8,18 @@
 TENSOR = ("tensor_0", "tensor_1")
 slope_const = 0.7978845608028654
 cubic_coef = 0.044715
+
+
+def fill_trails_now(vector, along_axis):
+    return jnp.concatenate(
+        jax.lax.all_to_all(
+            jnp.stack([vector for _ in range(jax.lax.axis_size(along_axis))], 0), along_axis, 0, 0
+        ),
+        1,
+    )
+
+
+point_the_members_all = functools.partial(fill_trails_now, along_axis=TENSOR)
 
 
 def in_order(pieces, dim):
@@ -150,7 +163,7 @@
     wf_down = down_fake[0]
     real_pos = slot_index(routes_real, experts, capacity)
     real_pick = spread_matrix(real_pos, total)
-    whole = lax.all_gather(x_real, TENSOR, axis=1, tiled=True)
+    whole = point_the_members_all(x_real)
     fake_pos = slot_index(routes_fake, experts, capacity)
     fake_pick = spread_matrix(fake_pos, total)
     fake_flat = pick_matrix(fake_pos, total)

time: 433 us -> 386 us (0.89)
  waiting for transfers between devices: 252 us -> 185 us
  starting transfers between devices: 15.4 us -> 26.3 us
  blocking collectives: 94.8 us -> 100 us
    all_gather x1 -> x0, waiting for transfers between devices: 55.5 us -> none  [on_device(): whole = lax.all_gather(x_real, TENSOR, axis=1, tiled=True)]
    all_gather x1, waiting for transfers between devices: 150 us -> 103 us  [on_device(): both = lax.all_gather(both, TENSOR, axis=1, tiled=True)]
    all_to_all x0 -> x1, waiting for transfers between devices: none -> 21 us  [fill_trails_now(): jax.lax.all_to_all(jnp.stack([vector for _ in range(jax.lax.axis_size(alo...]
    reduce_scatter x2, waiting for transfers between devices: 39.7 us -> 52.3 us  [reduced_to_own(): pieces = lax.psum_scatter(pieces, axes[k], scatter_dimension=0, tiled=True)]
    all_to_all x0 -> x1, starting transfers between devices: none -> 10.6 us  [fill_trails_now(): jax.lax.all_to_all(jnp.stack([vector for _ in range(jax.lax.axis_size(alo...]
  transfers between devices with their start and end apart: 9 -> 9, of which waited for: 4 -> 4; matrix products, arithmetic and copies ran while one was open for 8% -> 7% of each run, Pallas kernels for 0% -> 0%
where the time goes in v1:
time: 386 us; the launch traced here: 385 us
  waiting for transfers between devices  185 us (48%)
  blocking collectives  100 us (26%)
  matrix products  36.4 us (9%)
  starting transfers between devices  26.3 us (7%)
  between operations  15.8 us (4%)
  local copies, waits for them, and re-layouts  13.3 us (3%)
  other arithmetic  8.71 us (2%)
    all_gather x1, waiting for transfers between devices, on_device(): both = lax.all_gather(both, TENSOR, axis=1, tiled=True)  103 us
    reduce_scatter x2, waiting for transfers between devices, reduced_to_own(): pieces = lax.psum_scatter(pieces, axes[k], scatter_dimension=0, tiled=True)  52.3 us
    all_to_all x1, blocking collectives, on_device(): lax.all_to_all(sent, 'expert', split_axis=0, concat_axis=0, tiled=True)  50.6 us
    all_to_all x1, blocking collectives, on_device(): lax.all_to_all(partial_out.reshape(experts, capacity, width), 'expert', s...  49.3 us
    all_to_all x1, waiting for transfers between devices, fill_trails_now(): jax.lax.all_to_all(jnp.stack([vector for _ in range(jax.lax.axis_size(alo...  21 us
    dot_general x4, matrix products, over_rows(): lax.dot_general(left, right, (((0,), (0,)), ((), ())), preferred_element_...  12.7 us
    all_to_all x1, starting transfers between devices, fill_trails_now(): jax.lax.all_to_all(jnp.stack([vector for _ in range(jax.lax.axis_size(alo...  10.6 us
    dot_general x1, matrix products, on_device(): jnp.dot(hidden, w_down, preferred_element_type=jnp.float32)  9.62 us
  transfers between devices with their start and end apart: 9, of which 4 were waited for; matrix products, arithmetic and copies ran while one was open for 7% of the time, Pallas kernels for 0%

profile of v1, /device:TPU:1, one launch (start us, length us, event | category | flops | bytes accessed | tf_op | source)
XLA Modules:
  0.0 385.4 jit_solution(541823334545403023)
XLA Ops:
  8.0 0.0 copy-start
  8.0 0.8 convert_reduce_fusion.2
  8.9 0.6 reduce-window.16
  9.4 0.2 slice_reduce_fusion
  9.7 0.1 bitcast_subtract_fusion
  9.8 0.7 select_reduce_fusion.1
  10.5 0.7 multiply_add_fusion.2
  11.1 0.1 copy.32
  11.3 0.3 convert_reduce_fusion
  11.6 0.1 eq.86
  11.7 0.8 copy.33
  12.5 0.1 mul.132
  12.7 0.0 copy-start.8
  12.7 1.2 convolution_convert_fusion.2
  13.9 0.9 mul.134
  14.8 0.9 fusion.31
  15.7 0.8 pad_maximum_fusion
  16.5 6.0 %all-to-all-start.1 = ((bf16[8,256,128]{2,1,0:T(8,128)(2,1)}), bf16[8,256,128]{2,1,0:T(8,128)(2,1)S(1)}, u32[]{:S(2)}, u32[]{:S(2)}) async-start(bf16[8,256,128]{2,1,0:T(8,128)(2,1)} %pad_maximum_fusion), calls=%async_computation.1 | async-start | bytes 1048576 | tf_op jit(solution)/shard_map/all_to_all | solution.py:78
  22.5 0.1 copy.31
  22.6 8.6 %all-to-all-done.1 = bf16[8,256,128]{2,1,0:T(8,128)(2,1)S(1)} async-done(((bf16[8,256,128]{2,1,0:T(8,128)(2,1)}), bf16[8,256,128]{2,1,0:T(8,128)(2,1)S(1)}, u32[]{:S(2)}, u32[]{:S(2)}) %all-to-all-start.1) | async-done | bytes 524320 | tf_op jit(solution)/shard_map/all_to_all | solution.py:78
  31.2 1.1 stack.2
  32.4 10.6 %all-to-all-start = ((bf16[16,256,128]{1,2,0:T(8,128)(2,1)}), bf16[16,256,128]{1,2,0:T(8,128)(2,1)S(1)}, u32[]{:S(2)}, u32[]{:S(2)}) async-start(bf16[16,256,128]{1,2,0:T(8,128)(2,1)} %stack.2), calls=%async_computation | async-start | bytes 2097152 | tf_op jit(solution)/shard_map/all_to_all | solution.py:15
  43.0 0.0 reduce-scatter.3.cloned.1.call-start
  43.1 0.6 reduce-window.14
  43.7 0.2 slice_reduce_fusion.1
  43.9 0.1 bitcast_subtract_fusion.1
  44.1 1.6 select_reduce_fusion
  45.6 1.1 fusion.50
  46.7 0.9 pad_maximum_fusion.1
  47.6 21.0 %all-to-all-done = bf16[16,256,128]{1,2,0:T(8,128)(2,1)S(1)} async-done(((bf16[16,256,128]{1,2,0:T(8,128)(2,1)}), bf16[16,256,128]{1,2,0:T(8,128)(2,1)S(1)}, u32[]{:S(2)}, u32[]{:S(2)}) %all-to-all-start) | async-done | bytes 1048608 | tf_op jit(solution)/shard_map/all_to_all | solution.py:15
  68.6 2.4 convolution_convert_fusion.1
  71.0 50.6 %all_to_all.20 = bf16[8,128,2048]{2,1,0:T(8,128)(2,1)} all-to-all(bf16[8,128,2048]{2,1,0:T(8,128)(2,1)S(1)} %bitcast.75), channel_id=1, replica_groups=mesh['expert'=8,'tensor_0'=2,'tensor_1'=8,'dp'=2] {'expert'}, dimensions={0} | all-to-all | bytes 8388608 | tf_op jit(solution)/shard_map/all_to_all | solution.py:184
  121.6 9.6 %convolution_convert_fusion = bf16[1024,2048]{1,0:T(8,128)(2,1)} fusion(bf16[1,512,2048]{2,1,0:T(8,128)(2,1)S(1)} %copy-done, bf16[1024,2048]{1,0:T(8,128)(2,1)} %bitcast.81, bf16[1,2048,512]{2,1,0:T(8,128)(2,1)} %param.14), kind=kOutput, calls=%fused_computation | convolution fusion | flops 4301783040 | bytes 12582912 | tf_op jit(solution)/shard_map/dot_general | solution.py:188
  131.2 49.3 %all_to_all.21 = bf16[8,128,2048]{2,1,0:T(8,128)(2,1)S(1)} all-to-all(bf16[8,128,2048]{2,1,0:T(8,128)(2,1)} %bitcast.82), channel_id=1, replica_groups=mesh['expert'=8,'tensor_0'=2,'tensor_1'=8,'dp'=2] {'expert'}, dimensions={0} | all-to-all | bytes 8388608 | tf_op jit(solution)/shard_map/all_to_all | solution.py:189
  180.6 1.3 fusion.38
  181.8 1.3 fusion.24
  183.2 0.4 copy.35
  183.6 2.0 copy.34
  185.6 0.0 reduce-scatter.3.cloned.1.call-update
  185.6 0.0 all-gather.2.cloned.1.call-start
  185.7 0.5 all-gather.2.cloned.1.call-update
  186.2 0.2 reduce-scatter.5.cloned.1.call-start
  186.4 52.3 %reduce-scatter.3.cloned.1.call-done = f32[2,256,128]{2,1,0:T(8,128)} async-done(((f32[16,256,128]{2,1,0:T(8,128)}), f32[2,256,128]{2,1,0:T(8,128)}) %reduce-scatter.3.cloned.1.call-update) | async-done | bytes 262160 | tf_op jit(solution)/shard_map/reduce_scatter | solution.py:46
  238.7 0.0 reduce-scatter.5.cloned.1.call-update
  238.8 102.5 %all-gather.2.cloned.1.call-done = bf16[2048,2048]{1,0:T(8,128)(2,1)} async-done(((bf16[2048,128]{1,0:T(8,128)(2,1)}), bf16[2048,2048]{1,0:T(8,128)(2,1)}) %all-gather.2.cloned.1.call-update) | async-done | bytes 8388624 | tf_op jit(solution)/shard_map/all_gather | solution.py:180
  341.3 4.1 %fusion.49 = (bf16[1024,2048]{1,0:T(8,128)(2,1)S(1)}, bf16[1024,2048]{1,0:T(8,128)(2,1)S(1)}) fusion(bf16[2048,2048]{1,0:T(8,128)(2,1)} %all-gather.2.cloned.1.call-done), kind=kLoop, calls=%fused_computation.78 | loop fusion | bytes 16777216 | tf_op jit(solution)/shard_map/slice | solution.py:181
  345.4 0.2 constant_dynamic-slice_fusion.1
  345.7 4.3 %collective-permute-start = (bf16[1024,1024]{1,0:T(8,128)(2,1)S(1)}, bf16[1024,1024]{1,0:T(8,128)(2,1)}, u32[]{:S(2)}, u32[]{:S(2)}) collective-permute-start(bf16[1024,1024]{1,0:T(8,128)(2,1)S(1)} %constant_dynamic-slice_fusion.1), channel_id=1, source_target_pairs={{0,1},{1,0},{2,3},{3,2},{4,5},{5,4},{6,7},{7,6},{8,9},{9,8},{10,11... | collective-permute-start | bytes 6291464 | tf_op jit(solution)/shard_map/ppermute | solution.py:88
  349.9 1.6 constant_dynamic-slice_fusion
  351.5 1.8 collective-permute-start.3
  353.3 2.7 multiply_convert_fusion
  356.1 4.3 %fusion.11 = bf16[1024,512]{1,0:T(8,128)(2,1)} fusion(f32[1024,512]{1,0:T(8,128)S(1)} %get-tuple-element.14, bf16[1,512,2048]{2,1,0:T(8,128)(2,1)S(1)} %copy-done.12, bf16[2048,2048]{1,0:T(8,128)(2,1)S(1)} %copy-done.5), kind=kOutput, calls=%fused_computation.17 | convolution fusion | flops 2157445120 | bytes 9437184 | tf_op jit(solution)/shard_map/dot_general | solution.py:207
  360.3 3.3 collective-permute-start.1
  363.6 1.5 convert_bitcast_fusion
  365.2 0.0 collective-permute-start.2
  365.2 3.3 fusion.21
  368.5 1.3 fusion.19
  369.8 0.0 collective-permute-done.1
  369.8 0.0 collective-permute-done
  369.8 0.0 copy-start.1
  369.8 4.3 %fusion.25 = bf16[1,1024,512]{2,1,0:T(8,128)(2,1)} fusion(f32[1024,512]{1,0:T(8,128)S(1)} %fusion.21, bf16[1024,1024]{1,0:T(8,128)(2,1)} %collective-permute-done, bf16[1024,512]{1,0:T(8,128)(2,1)} %collective-permute-done.1), kind=kOutput, calls=%fused_computation.40 | convolution fusion | flops 1074790400 | bytes 6291456 | tf_op jit(solution)/shard_map/dot_general | solution.py:132
  374.1 0.0 collective-permute-done.2
  374.1 0.0 collective-permute-done.3
  374.1 3.9 %fusion.26 = bf16[1,512,1024]{2,1,0:T(8,128)(2,1)} fusion(f32[512,1024]{1,0:T(8,128)S(1)} %fusion.19, bf16[1024,512]{1,0:T(8,128)(2,1)S(1)} %collective-permute-done.2, bf16[1024,1024]{1,0:T(8,128)(2,1)} %collective-permute-done.3), kind=kOutput, calls=%fused_computation.41 | convolution fusion | flops 1074790400 | bytes 6291456 | tf_op jit(solution)/shard_map/dot_general | solution.py:132
  (31 shorter events, 0.2 us)
Async XLA Ops:
  8.0 113.6 %copy-start = (bf16[1,512,2048]{2,1,0:T(8,128)(2,1)S(1)}, bf16[1,512,2048]{2,1,0:T(8,128)(2,1)}, u32[]{:S(2)}) copy-start(bf16[1,512,2048]{2,1,0:T(8,128)(2,1)} %param.15) | copy-start | bytes 6291460
  12.7 9.9 %copy-start.8 = (bf16[256,128]{1,0:T(8,128)(2,1)S(1)}, bf16[256,128]{1,0:T(8,128)(2,1)}, u32[]{:S(2)}) copy-start(bf16[256,128]{1,0:T(8,128)(2,1)} %param.11) | copy-start | bytes 196612
  16.5 26.5 %copy-start.9 = (s32[256,2]{0,1:T(2,128)S(1)}, s32[256,2]{0,1:T(2,128)}, u32[]{:S(2)}) copy-start(s32[256,2]{0,1:T(2,128)} %param.12) | copy-start | bytes 6148
  16.5 27.5 %copy-start.10 = (f32[256,2]{0,1:T(2,128)S(1)}, f32[256,2]{0,1:T(2,128)}, u32[]{:S(2)}) copy-start(f32[256,2]{0,1:T(2,128)} %param.13) | copy-start | bytes 6148
  16.5 14.7 %all-to-all-start.1 = ((bf16[8,256,128]{2,1,0:T(8,128)(2,1)}), bf16[8,256,128]{2,1,0:T(8,128)(2,1)S(1)}, u32[]{:S(2)}, u32[]{:S(2)}) async-start(bf16[8,256,128]{2,1,0:T(8,128)(2,1)} %pad_maximum_fusion), calls=%async_computation.1 | async-start | bytes 1048576 | tf_op jit(solution)/shard_map/all_to_all | solution.py:78
  31.2 1.1 copy-start.7
  32.4 36.2 %all-to-all-start = ((bf16[16,256,128]{1,2,0:T(8,128)(2,1)}), bf16[16,256,128]{1,2,0:T(8,128)(2,1)S(1)}, u32[]{:S(2)}, u32[]{:S(2)}) async-start(bf16[16,256,128]{1,2,0:T(8,128)(2,1)} %stack.2), calls=%async_computation | async-start | bytes 2097152 | tf_op jit(solution)/shard_map/all_to_all | solution.py:15
  43.0 195.7 %reduce-scatter.3.cloned.1.call-start = ((), (), s32[]{:S(2)}) async-start(), calls=%async_computation.6 | async-start | bytes 2359296 | tf_op jit(solution)/shard_map/reduce_scatter | solution.py:46
  131.2 49.3 %copy-start.6 = (f32[256,1024]{1,0:T(8,128)S(1)}, f32[256,1024]{1,0:T(8,128)}, u32[]{:S(2)}) copy-start(f32[256,1024]{1,0:T(8,128)} %get-tuple-element.7) | copy-start | bytes 3145732
  185.6 155.7 %all-gather.2.cloned.1.call-start = ((), (), s32[]{:S(2)}) async-start(), calls=%async_computation.8 | async-start | bytes 8912896 | tf_op jit(solution)/shard_map/all_gather | solution.py:180
  186.2 177.4 %reduce-scatter.5.cloned.1.call-start = ((), (), s32[]{:S(2)}) async-start(), calls=%async_computation.7 | async-start | bytes 393216 | tf_op jit(solution)/shard_map/reduce_scatter | solution.py:46
  341.3 12.0 %copy-start.11 = (bf16[1,2048,512]{2,1,0:T(8,128)(2,1)S(1)}, bf16[1,2048,512]{2,1,0:T(8,128)(2,1)}, u32[]{:S(2)}) copy-start(bf16[1,2048,512]{2,1,0:T(8,128)(2,1)} %param.20) | copy-start | bytes 6291460
  345.4 4.5 %copy-start.2 = (bf16[1024,2048]{1,0:T(8,128)(2,1)}, bf16[1024,2048]{1,0:T(8,128)(2,1)S(1)}, u32[]{:S(2)}) copy-start(bf16[1024,2048]{1,0:T(8,128)(2,1)S(1)} %get-tuple-element.9) | copy-start | bytes 12582916
  345.4 10.6 %copy-start.4 = (bf16[1024,2048]{1,0:T(8,128)(2,1)}, bf16[1024,2048]{1,0:T(8,128)(2,1)S(1)}, u32[]{:S(2)}) copy-start(bf16[1024,2048]{1,0:T(8,128)(2,1)S(1)} %get-tuple-element.10) | copy-start | bytes 12582916
  345.4 7.9 %copy-start.5 = (bf16[2048,2048]{1,0:T(8,128)(2,1)S(1)}, bf16[2048,2048]{1,0:T(8,128)(2,1)}, u32[]{:S(2)}) copy-start(bf16[2048,2048]{1,0:T(8,128)(2,1)} %all-gather.2.cloned.1.call-done) | copy-start | bytes 25165828
  345.7 24.1 %collective-permute-start = (bf16[1024,1024]{1,0:T(8,128)(2,1)S(1)}, bf16[1024,1024]{1,0:T(8,128)(2,1)}, u32[]{:S(2)}, u32[]{:S(2)}) collective-permute-start(bf16[1024,1024]{1,0:T(8,128)(2,1)S(1)} %constant_dynamic-slice_fusion.1), channel_id=1, source_target_pairs={{0,1},{1,0},{2,3},{3,2},{4,5},{5,4},{6,7},{7,6},{8,9},{9,8},{10,11... | collective-permute-start | bytes 6291464 | tf_op jit(solution)/shard_map/ppermute | solution.py:88
  351.5 4.5 %copy-start.12 = (bf16[1,512,2048]{2,1,0:T(8,128)(2,1)S(1)}, bf16[1,512,2048]{2,1,0:T(8,128)(2,1)}, u32[]{:S(2)}) copy-start(bf16[1,512,2048]{2,1,0:T(8,128)(2,1)} %param.21) | copy-start | bytes 6291460
  351.5 22.6 %collective-permute-start.3 = (bf16[1024,1024]{1,0:T(8,128)(2,1)}, bf16[1024,1024]{1,0:T(8,128)(2,1)}, u32[]{:S(2)}, u32[]{:S(2)}) collective-permute-start(bf16[1024,1024]{1,0:T(8,128)(2,1)} %constant_dynamic-slice_fusion), channel_id=1, source_target_pairs={{0,1},{1,0},{2,3},{3,2},{4,5},{5,4},{6,7},{7,6},{8,9},{9,8},{10,11... | collective-permute-start | bytes 6291464 | tf_op jit(solution)/shard_map/ppermute | solution.py:88
  360.3 9.4 %collective-permute-start.1 = (bf16[1024,512]{1,0:T(8,128)(2,1)}, bf16[1024,512]{1,0:T(8,128)(2,1)}, u32[]{:S(2)}, u32[]{:S(2)}) collective-permute-start(bf16[1024,512]{1,0:T(8,128)(2,1)} %fusion.11), channel_id=1, source_target_pairs={{0,1},{1,0},{2,3},{3,2},{4,5},{5,4},{6,7},{7,6},{8,9},{9,8},{10,11... | collective-permute-start | bytes 3145736 | tf_op jit(solution)/shard_map/ppermute | solution.py:88
  365.2 3.3 copy-start.3
  365.2 8.9 %collective-permute-start.2 = (bf16[1024,512]{1,0:T(8,128)(2,1)S(1)}, bf16[1024,512]{1,0:T(8,128)(2,1)S(1)}, u32[]{:S(2)}, u32[]{:S(2)}) collective-permute-start(bf16[1024,512]{1,0:T(8,128)(2,1)S(1)} %get-tuple-element.13), channel_id=1, source_target_pairs={{0,1},{1,0},{2,3},{3,2},{4,5},{5,4},{6,7},{7,6},{8,9},{9,8},{10,11... | collective-permute-start | bytes 3145736 | tf_op jit(solution)/shard_map/ppermute | solution.py:88
  369.8 8.1 %copy-start.1 = (bf16[1,512,2048]{2,1,0:T(8,128)(2,1)S(1)}, bf16[1,512,2048]{2,1,0:T(8,128)(2,1)}, u32[]{:S(2)}) copy-start(bf16[1,512,2048]{2,1,0:T(8,128)(2,1)} %param.15) | copy-start | bytes 6291460
Sparse Core Ops, SparseCore 0:
  185.7 52.9 reduce-scatter.2
  241.2 22.5 reduce-scatter.4
Sparse Core Ops, SparseCore 1:
  188.6 152.6 all-gather.1
